TPU v7x, 32 devices: a whole 2x2x4 slice. The times are simulated.
32 devices in a mesh: dop: 8 (over z, y), slow: 4 (over x, core).
Axes of the slice: x: 2, y: 2, z: 4, core: 2. Of those that a mesh axis runs over, the one named last changes fastest.
Arguments:
- profiles: bfloat16 [32, 2, 1024, 2048], P('slow', None, 'dop'), may hold values from -6 to 6
- range_walk: int32 [2048], replicated, may hold values from -32 to 32
- band_order: int32 [32], replicated, may hold values from 0 to 31, each once
Outputs:
- ambiguity: float32 [2048, 1024], P(('dop', 'slow'))
Inputs may be any that keep to these rules, and one draw needn't show every extreme that they name: `band_order`: each band number appears exactly once.
All inputs are finite; a program needn't handle non-finite values.
Results may differ from a plain program's by a relative error of at most 0.00067.
Values sent between devices are 32-bit elements; how exact they have to be, the bound alone decides.
A program may use at most 128 MiB of HBM per device.

v0:
```python
import functools
import math

import jax
import jax.numpy as jnp
import numpy as np
from jax import lax
from jax.experimental import pallas as pl
from jax.experimental.pallas import tpu as pltpu
from jax.sharding import PartitionSpec as P

WALK = 32
LANES = 128
TILE = 16
RADIX = 4


def rotation(rows, pulses, length):
    phases = (np.asarray(rows)[..., None] * np.arange(pulses)) % length
    angles = phases * (2.0 * math.pi / length)
    return np.cos(angles).astype(np.float32), np.sin(angles).astype(np.float32)


def quarter_sums(x_ref, at, short):
    re = [x_ref[at, 0, :, q * short:(q + 1) * short].astype(jnp.float32) for q in range(RADIX)]
    im = [x_ref[at, 1, :, q * short:(q + 1) * short].astype(jnp.float32) for q in range(RADIX)]
    are, aim, bre, bim = re[0] + re[2], im[0] + im[2], re[0] - re[2], im[0] - im[2]
    cre, cim, dre, dim = re[1] + re[3], im[1] + im[3], re[1] - re[3], im[1] - im[3]
    return (
        (are + cre, aim + cim),
        (bre + dim, bim - dre),
        (are - cre, aim - cim),
        (bre - dim, bim + dre),
    )


def power_kernel(
    batch_count, total_batches, per_band, scale, joined,
    order_ref, x_ref, walk_ref, turns, *refs,
):
    *outs, table, packed, own_sum, rim_sum, walks = refs
    step = pl.program_id(0)
    short = x_ref.shape[3] // RADIX
    bins = table.shape[1]
    base_rows = max(per_band, TILE)
    bands_at = RADIX * base_rows

    @pl.when(step == 0)
    def _():
        own_sum[...] = jnp.zeros_like(own_sum)
        rim_sum[...] = jnp.zeros_like(rim_sum)
        row = lax.broadcasted_iota(jnp.int32, (TILE, short), 0) // min(per_band, TILE)

        @pl.loop(0, bins // TILE)
        def _(tile):
            start = pl.multiple_of(tile * TILE, TILE)
            first = start // per_band
            inside = pl.multiple_of(start % per_band, TILE) if per_band > TILE else 0
            vc = turns[0, pl.ds(bands_at + order_ref[first], 1), :]
            vs = turns[1, pl.ds(bands_at + order_ref[first], 1), :]
            for extra in range(1, max(1, TILE // per_band)):
                band = order_ref[first + extra]
                vc = jnp.where(row == extra, turns[0, pl.ds(bands_at + band, 1), :], vc)
                vs = jnp.where(row == extra, turns[1, pl.ds(bands_at + band, 1), :], vs)
            for r in range(RADIX):
                if joined:
                    at = order_ref[first] * (per_band * RADIX) + inside * RADIX + r
                    walks[r, pl.ds(start, TILE), :] = walk_ref[pl.ds(at, TILE, stride=RADIX), :]
                else:
                    walks[r, pl.ds(start, TILE), :] = walk_ref[r, pl.ds(start, TILE), :]
                bc = turns[0, pl.ds(r * base_rows + inside, TILE), :]
                bs = turns[1, pl.ds(r * base_rows + inside, TILE), :]
                table[r, pl.ds(start, TILE), :short] = (bc * vc - bs * vs).astype(jnp.bfloat16)
                table[r, pl.ds(start, TILE), short:] = (bs * vc + bc * vs).astype(jnp.bfloat16)

    each = x_ref.shape[0]
    batch = lax.axis_index("slow") * batch_count + step * each
    lane = lax.broadcasted_iota(jnp.int32, (bins, LANES), 1)
    for at in range(each):
        top, low = 2 * LANES * at, 2 * LANES * at + LANES
        for r, parts in enumerate(quarter_sums(x_ref, at, short)):
            yre, yim = (part.astype(jnp.bfloat16) for part in parts)
            packed[r, top:low, :short] = yre
            packed[r, top:low, short:] = yim
            packed[r, low:low + LANES, :short] = yim
            packed[r, low:low + LANES, short:] = -yre

    def align(r, spec):
        own_add, rim_add = 0.0, 0.0
        for at in range(each):
            re = spec[:, 2 * LANES * at:2 * LANES * at + LANES]
            im = spec[:, 2 * LANES * at + LANES:2 * LANES * (at + 1)]
            power = re * re + im * im
            moved = walks[r] * (batch + at)
            if power_of_two(total_batches):
                offset = lax.shift_right_arithmetic(moved, total_batches.bit_length() - 1)
            else:
                offset = jnp.floor_divide(moved, total_batches)
            source = lane + offset
            wrapped = source & (LANES - 1)
            value = jnp.take_along_axis(power, wrapped, axis=1, mode="promise_in_bounds")
            inside = source == wrapped
            own_add += jnp.where(inside, value, 0.0)
            rim_add += jnp.where(inside, 0.0, value)
        own_sum[r] += own_add
        rim_sum[r] += rim_add

    pending = None
    for r in range(RADIX):
        spec = lax.dot_general(
            table[r], packed[r], (((1,), (1,)), ((), ())), preferred_element_type=jnp.float32
        )
        if pending is not None:
            align(r - 1, pending)
        pending = spec
    align(RADIX - 1, pending)

    @pl.when(step == pl.num_programs(0) - 1)
    def _():
        if joined:
            out_ref = outs[0]
            band_rows = per_band * RADIX
            half = band_rows // 2

            @pl.loop(0, bins // per_band)
            def _(block):
                rows = pl.ds(pl.multiple_of(block * per_band, per_band), per_band)
                for r in range(RADIX):
                    out_ref[block, pl.ds(r, per_band, stride=RADIX), :] = rim_sum[r, rows, :] * scale
                low, high = out_ref[block, :half, :], out_ref[block, half:band_rows, :]
                out_ref[block, band_rows:, :] = low + pltpu.roll(high, LANES // 2, 1)
                for r in range(RADIX):
                    out_ref[block, pl.ds(r, per_band, stride=RADIX), :] = own_sum[r, rows, :] * scale
        else:
            for r in range(RADIX):
                outs[0][pl.ds(r, bins, stride=RADIX), :] = own_sum[r] * scale
                outs[1][pl.ds(r, bins, stride=RADIX), :] = rim_sum[r] * scale


def aligned_power(profiles, range_walk, band_order, total_batches, joined):
    batch_count, _, delays, pulses = profiles.shape
    band_count = band_order.shape[0]
    band_rows = pulses // band_count
    per_band = band_rows // RADIX
    bins, short = pulses // RADIX, pulses // RADIX
    scale = 1.0 / (total_batches * pulses)
    if delays < LANES:
        profiles = jnp.pad(profiles, ((0, 0), (0, 0), (0, LANES - delays), (0, 0)))
    if joined:
        walks = jnp.broadcast_to(range_walk[:, None], (pulses, LANES))
    else:
        picked = band_order[:, None, None] == jnp.arange(band_count, dtype=jnp.int32)[None, :, None]
        walks = jnp.sum(jnp.where(picked, range_walk.reshape(1, band_count, band_rows), 0), axis=1)
        walks = jnp.broadcast_to(walks.reshape(bins, RADIX).T[:, :, None], (RADIX, bins, LANES))
    each = 2 if batch_count % 2 == 0 else 1
    inner = np.arange(max(per_band, TILE)) % per_band
    base = (RADIX * inner[None, :] + np.arange(RADIX)[:, None]).reshape(-1)
    band = np.arange(band_count) * band_rows
    turns = np.stack(rotation(np.concatenate([base, band]), short, pulses))
    whole = lambda shape: pl.BlockSpec(shape, lambda g, order: (0,) * len(shape))
    if joined:
        shapes = ((band_count, band_rows + band_rows // 2, LANES),)
    else:
        shapes = ((pulses, LANES),) * 2
    return pl.pallas_call(
        functools.partial(power_kernel, batch_count, total_batches, per_band, scale, joined),
        out_shape=[jax.ShapeDtypeStruct(shape, jnp.float32) for shape in shapes],
        grid_spec=pltpu.PrefetchScalarGridSpec(
            num_scalar_prefetch=1,
            grid=(batch_count // each,),
            in_specs=[
                pl.BlockSpec((each, 2, LANES, pulses), lambda g, order: (g, 0, 0, 0)),
                whole(walks.shape),
                whole(turns.shape),
            ],
            out_specs=[whole(shape) for shape in shapes],
            scratch_shapes=[
                pltpu.VMEM((RADIX, bins, 2 * short), jnp.bfloat16),
                pltpu.VMEM((RADIX, 2 * LANES * each, 2 * short), jnp.bfloat16),
                pltpu.VMEM((RADIX, bins, LANES), jnp.float32),
                pltpu.VMEM((RADIX, bins, LANES), jnp.float32),
                pltpu.VMEM((RADIX, bins, LANES), jnp.int32),
            ],
        ),
        compiler_params=pltpu.CompilerParams(
            dimension_semantics=("arbitrary",), vmem_limit_bytes=48 << 20
        ),
    )(band_order, profiles, walks, jnp.asarray(turns))


MESH = pl.DeviceIdType.MESH


def bit_of(value, k):
    return lax.rem(lax.div(value, 1 << k), 2)


def flipped(value, mask):
    result = value
    for k in range(mask.bit_length()):
        if mask >> k & 1:
            result = result + (1 << k) * (1 - 2 * bit_of(value, k))
    return result


def regroup_kernel(dop_count, slow_count, data, out_ref, *refs):
    levels = slow_count.bit_length() - 1
    kept, arrived = refs[:levels], refs[levels:2 * levels]
    landed, send_sem, recv_sem = refs[2 * levels:]
    dop, slow = lax.axis_index("dop"), lax.axis_index("slow")
    band_rows = out_ref.shape[0]
    partners = [(dop, flipped(slow, 1 << k)) for k in range(levels)]
    partners += [(flipped(dop, j), slow) for j in range(1, dop_count)]

    barrier = pltpu.get_barrier_semaphore()
    for partner in partners:
        pl.semaphore_signal(barrier, inc=1, device_id=partner, device_id_type=MESH)
    pl.semaphore_wait(barrier, len(partners))

    order = list(range(dop_count - 1, -1, -1))
    copies = {}

    def send(level, j, source, target, device):
        copies[level, j] = pltpu.make_async_remote_copy(
            src_ref=source, dst_ref=target,
            send_sem=send_sem.at[level, j], recv_sem=recv_sem.at[level, j],
            device_id=device, device_id_type=MESH,
        )
        copies[level, j].start()

    for j in order:
        send(0, j, data.at[flipped(dop, j), :, 1 - bit_of(slow, 0)], arrived[0].at[j], partners[0])
    for level in range(levels):
        for j in order:
            copies[level, j].wait_recv()
            bit = bit_of(slow, level)
            held = data[flipped(dop, j), :, bit] if level == 0 else kept[level - 1][j, :, bit]
            total = held + arrived[level][j]
            if level < levels - 1:
                kept[level][j] = total.reshape(kept[level].shape[1:])
                send(
                    level + 1, j, kept[level].at[j, :, 1 - bit_of(slow, level + 1)],
                    arrived[level + 1].at[j], partners[level + 1],
                )
            elif j:
                kept[level][j] = total[0]
                send(levels, j, kept[level].at[j], landed.at[j], (flipped(dop, j), slow))
            else:
                landed[0] = total[0]
    for j in order[:-1]:
        copies[levels, j].wait_recv()

    half = band_rows // 2
    lane = lax.broadcasted_iota(jnp.int32, (half, LANES), 1)
    for e in range(dop_count):
        main = landed[flipped(dop, e), :band_rows, :]
        low = jnp.zeros((half, LANES), jnp.float32)
        high = low
        for source, mine in ((e - 1, lane < WALK), (e + 1, lane >= LANES - WALK)):
            if 0 <= source < dop_count:
                rim = landed[flipped(dop, source), band_rows:, :]
                low += jnp.where(mine, rim, 0.0)
                high += jnp.where(mine, pltpu.roll(rim, LANES // 2, 1), 0.0)
        out_ref[:half, e * LANES:(e + 1) * LANES] = main[:half] + low
        out_ref[half:, e * LANES:(e + 1) * LANES] = main[half:] + high
    for copy in copies.values():
        copy.wait_send()


def regroup(blocks, dop_count, slow_count):
    rows = blocks.shape[1]
    band_rows = rows // 3 * 2
    levels = slow_count.bit_length() - 1
    kept, arrived = [], []
    count = slow_count
    for level in range(levels):
        count //= 2
        pair = (count // 2, 2) if count > 1 else ()
        kept.append(pltpu.VMEM((dop_count, *pair, rows, LANES), jnp.float32))
        arrived.append(pltpu.VMEM((dop_count, count, rows, LANES), jnp.float32))
    return pl.pallas_call(
        functools.partial(regroup_kernel, dop_count, slow_count),
        out_shape=jax.ShapeDtypeStruct((band_rows, dop_count * LANES), jnp.float32),
        in_specs=[pl.BlockSpec(memory_space=pltpu.VMEM)],
        out_specs=pl.BlockSpec(memory_space=pltpu.VMEM),
        scratch_shapes=[
            *kept, *arrived,
            pltpu.VMEM((dop_count, rows, LANES), jnp.float32),
            pltpu.SemaphoreType.DMA((levels + 1, dop_count)),
            pltpu.SemaphoreType.DMA((levels + 1, dop_count)),
        ],
        compiler_params=pltpu.CompilerParams(
            collective_id=0, has_side_effects=True, vmem_limit_bytes=32 << 20
        ),
    )(blocks.reshape(dop_count, slow_count // 2, 2, rows, LANES))


def power_of_two(count):
    return count & (count - 1) == 0


def neighbours(value, steps):
    count = lax.axis_size("dop")
    pairs = [(source, source + steps) for source in range(count) if 0 <= source + steps < count]
    return lax.ppermute(value, "dop", pairs)


def exchange(own, rim, delays):
    dop_count, slow_count = lax.axis_size("dop"), lax.axis_size("slow")
    rows = own.shape[0] // (dop_count * slow_count)
    after = rim[:, :WALK] if delays == LANES else own[:, delays:delays + WALK]
    from_below = neighbours(after, 1)
    from_above = neighbours(rim[:, LANES - WALK:], -1)
    own = own[:, :delays].at[:, :WALK].add(from_below)
    own = own.at[:, delays - WALK:].add(from_above)
    grouped = own.reshape(dop_count, slow_count, rows, delays)
    summed = lax.psum_scatter(grouped, "slow", scatter_dimension=1, tiled=False)
    gathered = lax.all_to_all(summed, "dop", split_axis=0, concat_axis=0, tiled=True)
    return gathered.transpose(1, 0, 2).reshape(rows, dop_count * delays)


def on_device(profiles, range_walk, band_order):
    total_batches = profiles.shape[0] * lax.axis_size("slow")
    delays = profiles.shape[2]
    dop_count, slow_count = lax.axis_size("dop"), lax.axis_size("slow")
    per_band = profiles.shape[3] // (dop_count * slow_count * RADIX)
    joined = (
        delays == LANES and per_band % TILE == 0 and slow_count > 1
        and power_of_two(dop_count) and power_of_two(slow_count)
    )
    sums = aligned_power(profiles, range_walk, band_order, total_batches, joined)
    if joined:
        return regroup(sums[0], dop_count, slow_count)
    return exchange(*sums, delays)


def solution(mesh):
    placed = (P("slow", None, "dop", None), P(), P())
    return jax.shard_map(
        on_device, mesh=mesh, in_specs=placed, out_specs=P(("dop", "slow"), None), check_vma=False
    )
```

profile of v0, /device:TPU:0, one launch (start us, length us, event | category | flops | bytes accessed | tf_op | source)
XLA Modules:
  0.0 42.8 jit_solution(11370458590853907184)
XLA Ops:
  0.0 1.0 %broadcast_in_dim.2.walk_ref = s32[2048,128]{1,0:T(8,128)S(1)} broadcast(s32[2048]{0:T(1024)} %param.5), dimensions={0} | broadcast | bytes 1056768 | tf_op jit(solution)/shard_map/broadcast_in_dim | solution.py:150
  1.0 0.0 copy-start
  1.0 1.0 %copy-done = f32[2,96,512]{2,1,0:T(8,128)S(1)} copy-done((f32[2,96,512]{2,1,0:T(8,128)S(1)}, f32[2,96,512]{2,1,0:T(8,128)}, u32[]{:S(2)}) %copy-start) | copy-done | bytes 393240
  2.0 0.0 copy-start.1
  2.0 0.7 %copy-done.1 = s32[32]{0:T(128)S(1)} copy-done((s32[32]{0:T(128)S(1)}, s32[32]{0:T(128)}, u32[]{:S(2)}) %copy-start.1) | copy-done | bytes 152
  2.7 18.1 %shard_map.46 = f32[32,96,128]{2,1,0:T(8,128)S(1)} custom-call(s32[32]{0:T(128)S(1)} %copy-done.1, bf16[8,2,128,2048]{3,2,1,0:T(8,128)(2,1)} %x_ref.1, s32[2048,128]{1,0:T(8,128)S(1)} %broadcast_in_dim.2.walk_ref, f32[2,96,512]{2,1,0:T(8,128)S(1)} %copy-done), custom_call_target="tpu_custom_call" | custom-call | tf_op jit(solution)/shard_map/pallas_call | solution.py:165
  20.8 21.4 %shard_map.47 = f32[64,1024]{1,0:T(8,128)S(1)} custom-call(f32[8,2,2,96,128]{4,3,2,1,0:T(8,128)S(1)} %bitcast.1), custom_call_target="tpu_custom_call" | custom-call | tf_op jit(solution)/shard_map/pallas_call | solution.py:281
  42.1 0.7 %copy.6 = f32[64,1024]{1,0:T(8,128)} copy(f32[64,1024]{1,0:T(8,128)S(1)} %shard_map.47) | data formatting | bytes 524288
Async XLA Ops:
  1.0 1.0 %copy-start = (f32[2,96,512]{2,1,0:T(8,128)S(1)}, f32[2,96,512]{2,1,0:T(8,128)}, u32[]{:S(2)}) copy-start(f32[2,96,512]{2,1,0:T(8,128)} %constant.2.clone.turns) | copy-start | bytes 1179652
  2.0 0.7 %copy-start.1 = (s32[32]{0:T(128)S(1)}, s32[32]{0:T(128)}, u32[]{:S(2)}) copy-start(s32[32]{0:T(128)} %order_ref.1) | copy-start | bytes 388
where the time goes:
time: 43 us; the launch traced here: 42.8 us
  Pallas kernels  39.4 us (92%)
  local copies, waits for them, and re-layouts  3.37 us (8%)
    pallas_call x1, Pallas kernels, regroup(): pl.pallas_call(functools.partial(regroup_kernel, dop_count, slow_count),...  21.4 us
    pallas_call x1, Pallas kernels, aligned_power(): pl.pallas_call(functools.partial(power_kernel, batch_count, total_batches...  18.1 us
    unnamed x5, local copies, waits for them, and re-layouts  2.35 us
    broadcast_in_dim x1, local copies, waits for them, and re-layouts, aligned_power(): walks = jnp.broadcast_to(range_walk[:, None], (pulses, LANES))  1.02 us

commit v1 on v0

--- a/solution.py
+++ b/solution.py
@@ -319,10 +319,341 @@
     return gathered.transpose(1, 0, 2).reshape(rows, dop_count * delays)
 
 
+FAN = 8
+SUB = 8
+PIECE = 32
+PAIR = 2
+
+
+def fan_table(pulses):
+    short = pulses // FAN
+    rows = (FAN * np.arange(short)[None, :] + np.arange(FAN)[:, None])[..., None]
+    phases = (rows * np.arange(short)) % pulses
+    angles = phases.astype(np.float32) * np.float32(2.0 * math.pi / pulses)
+    return jnp.asarray(np.concatenate([np.cos(angles), np.sin(angles)], axis=2), jnp.bfloat16)
+
+
+def turned(re, im):
+    half = math.sqrt(0.5)
+    are = [re[q] + re[q + 4] for q in range(4)]
+    aim = [im[q] + im[q + 4] for q in range(4)]
+    bre = [re[q] - re[q + 4] for q in range(4)]
+    bim = [im[q] - im[q + 4] for q in range(4)]
+    out = [None] * FAN
+    c0, c1, c2, c3 = are[0] + are[2], are[0] - are[2], are[1] + are[3], are[1] - are[3]
+    s0, s1, s2, s3 = aim[0] + aim[2], aim[0] - aim[2], aim[1] + aim[3], aim[1] - aim[3]
+    out[0], out[4] = (c0 + c2, s0 + s2), (c0 - c2, s0 - s2)
+    out[2], out[6] = (c1 + s3, s1 - c3), (c1 - s3, s1 + c3)
+    d0re, d0im, d1re, d1im = bre[0] + bim[2], bim[0] - bre[2], bre[0] - bim[2], bim[0] + bre[2]
+    p1, m1 = bre[1] + bim[1], bim[1] - bre[1]
+    p3, m3 = bre[3] + bim[3], bim[3] - bre[3]
+    e2re, e2im = (p1 + m3) * half, (m1 - p3) * half
+    e3re, e3im = (p1 - m3) * half, (m1 + p3) * half
+    out[1], out[5] = (d0re + e2re, d0im + e2im), (d0re - e2re, d0im - e2im)
+    out[3], out[7] = (d1re + e3im, d1im - e3re), (d1re - e3im, d1im + e3re)
+    return out
+
+
+def fused_body(
+    accs, dop_count, total_batches, scale,
+    x_hbm, table_hbm, walk_ref, order_ref, out_ref,
+    x_buf, table, minus, y_buf, spun, walks, own, rim, stage,
+    held, near, passed, across, last, landed,
+    x_sem, table_sem, near_send, near_recv, across_send, across_recv, land_send, land_recv,
+):
+    batches, _, delays, pulses = x_buf.shape
+    short = pulses // FAN
+    pairs = batches // PAIR
+    bands = order_ref.shape[0]
+    dop, slow = lax.axis_index("dop"), lax.axis_index("slow")
+    core, side = lax.rem(slow, 2), lax.div(slow, 2)
+    core_peer, side_peer = (dop, flipped(slow, 1)), (dop, flipped(slow, 2))
+    partners = [core_peer, side_peer] + [(flipped(dop, j), slow) for j in range(1, dop_count)]
+    groups = LANES // WALK
+    units = FAN + FAN // groups
+
+    loads = [pltpu.make_async_copy(x_hbm.at[g], x_buf.at[g], x_sem.at[g]) for g in range(batches)]
+    for load in loads:
+        load.start()
+    table_loads = [
+        pltpu.make_async_copy(table_hbm.at[r], table.at[r], table_sem.at[r]) for r in range(FAN)
+    ]
+    for load in table_loads:
+        load.start()
+
+    barrier = pltpu.get_barrier_semaphore()
+    for partner in partners:
+        pl.semaphore_signal(barrier, inc=1, device_id=partner, device_id_type=MESH)
+
+    for a in range(pulses // LANES):
+        row = jnp.broadcast_to(walk_ref[a:a + 1, :], (LANES, LANES))
+        spun[a * LANES:(a + 1) * LANES, :] = row.T
+    for r in range(FAN):
+        walks[r] = spun[pl.ds(r, short, stride=FAN), :].reshape(-1, SUB, LANES)
+
+    def spread(g):
+        @pl.loop(0, delays // 16)
+        def _(block):
+            at = pl.ds(pl.multiple_of(block * 16, 16), 16)
+            to = pl.ds(pl.multiple_of((g % PAIR) * delays + block * 16, 16), 16)
+            for lane in range(0, short, LANES):
+                parts = [
+                    [
+                        x_buf[g, c, at, q * short + lane:q * short + lane + LANES].astype(jnp.float32)
+                        for q in range(FAN)
+                    ]
+                    for c in range(2)
+                ]
+                for r, (re, im) in enumerate(turned(*parts)):
+                    y_buf[r, g // PAIR, to, lane:lane + LANES] = re.astype(jnp.bfloat16)
+                    y_buf[r, g // PAIR, to, short + lane:short + lane + LANES] = im.astype(jnp.bfloat16)
+
+    for g in range(batches):
+        loads[g].wait()
+        spread(g)
+
+    lane = lax.broadcasted_iota(jnp.int32, (PIECE, LANES), 1)
+    thin = lax.broadcasted_iota(jnp.int32, (SUB, LANES), 1)
+    shift = total_batches.bit_length() - 1
+    lanes = lane * total_batches
+    first_batch = slow * batches
+    pieces = short // PIECE
+
+    def align(r, half, piece, specs):
+        at = slice(piece * PIECE // SUB, (piece + 1) * PIECE // SUB)
+        walk = walks[r, at].reshape(PIECE, LANES)
+        own_add, rim_add = None, None
+        for q, (re, im) in enumerate(specs):
+            power = re * re + im * im
+            for b in range(PAIR):
+                batch = first_batch + (2 * half + q) * PAIR + b
+                source = lax.shift_right_arithmetic(lanes + walk * batch, shift)
+                wrapped = source & (LANES - 1)
+                value = jnp.take_along_axis(
+                    power[:, b * LANES:(b + 1) * LANES], wrapped, axis=1, mode="promise_in_bounds"
+                )
+                inside = source == wrapped
+                kept, spilled = jnp.where(inside, value, 0.0), jnp.where(inside, 0.0, value)
+                own_add = kept if own_add is None else own_add + kept
+                rim_add = spilled if rim_add is None else rim_add + spilled
+        if half:
+            own_add += own[r % 2, at].reshape(PIECE, LANES)
+            rim_add += rim[r % 2, at].reshape(PIECE, LANES)
+        own[r % 2, at] = own_add.reshape(-1, SUB, LANES)
+        rim[r % 2, at] = rim_add.reshape(-1, SUB, LANES)
+
+    def slot(band):
+        owner_dop, owner_slow = divmod(band, 4)
+        return owner_slow % 2, owner_dop, owner_slow // 2
+
+    copies = {}
+
+    def send(key, source, target, sent, received, device):
+        copies[key] = pltpu.make_async_remote_copy(
+            src_ref=source, dst_ref=target, send_sem=sent, recv_sem=received,
+            device_id=device, device_id_type=MESH,
+        )
+        copies[key].start()
+
+    def send_near(u):
+        send(("near", u), held.at[u, 1 - core], near.at[u], near_send.at[u], near_recv.at[u], core_peer)
+
+    def send_across(u):
+        copies["near", u].wait_recv()
+        for d in range(dop_count):
+            passed[u, d] = held[u, core, d, 1 - side] + near[u, d, 1 - side]
+        send(
+            ("across", u), passed.at[u], across.at[u], across_send.at[u], across_recv.at[u], side_peer
+        )
+
+    def send_home(u):
+        copies["across", u].wait_recv()
+        for j in range(dop_count - 1, -1, -1):
+            d = flipped(dop, j)
+            total = held[u, core, d, side] + near[u, d, side] + across[u, d]
+            if j:
+                last[u, j] = total
+                send(
+                    ("home", u, j), last.at[u, j], landed.at[u, j],
+                    land_send.at[u, j], land_recv.at[u, j], (d, slow),
+                )
+            else:
+                landed[u, 0] = total
+
+    def arrive(u):
+        for j in range(dop_count - 1, 0, -1):
+            copies["home", u, j].wait_recv()
+
+    def unit_of(r):
+        return r + r // groups
+
+    def put(r):
+        for e in range(dop_count):
+            stage[e, pl.ds(r, SUB, stride=FAN), :] = landed[unit_of(r), flipped(dop, e)]
+
+    def put_rim(h):
+        mine = order_ref[dop * 4 + slow]
+        u = h * (groups + 1) + groups
+        for k in range(groups):
+            r = h * groups + k
+            walk = walks[r, mine]
+            after = jnp.logical_and(walk < 0, thin < WALK)
+            before = jnp.logical_and(walk > 0, thin >= LANES - WALK)
+            for e in range(dop_count):
+                add = 0.0
+                for source, mask, move in ((e - 1, after, -k * WALK), (e + 1, before, LANES - WALK - k * WALK)):
+                    if 0 <= source < dop_count:
+                        value = landed[u, flipped(dop, source)]
+                        if move % LANES:
+                            value = pltpu.roll(value, move % LANES, 1)
+                        add = add + jnp.where(mask, value, 0.0)
+                at = (e, pl.ds(r, SUB, stride=FAN), slice(None))
+                stage[at] = stage[at] + add
+
+    def pack(r):
+        u = unit_of(r)
+        k = r % groups
+        for band in range(bands):
+            source = order_ref[band]
+            c, d, s = slot(band)
+            held[u, c, d, s] = own[r % 2, source] * scale
+            edge = rim[r % 2, source] * scale
+            left = pltpu.roll(edge, k * WALK, 1) if k else edge
+            right = pltpu.roll(edge, (k * WALK + WALK) % LANES, 1) if (k + 1) % groups else edge
+            mask = jnp.logical_and(thin >= k * WALK, thin < (k + 1) * WALK)
+            value = jnp.where(mask, left + right, 0.0)
+            v = (r // groups) * (groups + 1) + groups
+            held[v, c, d, s] = value if k == 0 else held[v, c, d, s] + value
+
+    for r in range(FAN):
+        table_loads[r].wait()
+        minus[...] = -table[r, :, :short]
+        for half in range(pairs // 2):
+            for q in range(2):
+                p = 2 * half + q
+                re_accs, im_accs = accs[q][half % 2]
+                pltpu.matmul_push_rhs(y_buf[r, p, :, :short], 0, q, transpose=True)
+                pltpu.matmul_push_rhs(y_buf[r, p, :, short:], 1, q, transpose=True)
+                for piece in range(pieces):
+                    rows = slice(piece * PIECE, (piece + 1) * PIECE)
+                    pltpu.matmul_acc_lhs(
+                        re_accs[piece], table[r, rows, :short], load_staged_rhs=0 if piece == 0 else None
+                    )
+                    pltpu.matmul_acc_lhs(im_accs[piece], table[r, rows, short:])
+                for piece in range(pieces):
+                    rows = slice(piece * PIECE, (piece + 1) * PIECE)
+                    pltpu.matmul_acc_lhs(
+                        re_accs[piece], table[r, rows, short:], load_staged_rhs=1 if piece == 0 else None
+                    )
+                    pltpu.matmul_acc_lhs(im_accs[piece], minus[rows, :])
+            for piece in range(pieces):
+                specs = []
+                for q in range(2):
+                    re_accs, im_accs = accs[q][half % 2]
+                    specs.append((pltpu.matmul_pop(re_accs[piece]), pltpu.matmul_pop(im_accs[piece])))
+                align(r, half, piece, specs)
+        pack(r)
+        if r == 0:
+            pl.semaphore_wait(barrier, len(partners))
+        send_near(unit_of(r))
+        if r % groups == groups - 1:
+            send_near(unit_of(r) + 1)
+        if r >= 1:
+            send_across(unit_of(r - 1))
+            if (r - 1) % groups == groups - 1:
+                send_across(unit_of(r - 1) + 1)
+
+    for u in range(unit_of(FAN - 1), units):
+        send_across(u)
+    for u in range(units):
+        send_home(u)
+    for h in range(FAN // groups):
+        for k in range(groups):
+            r = h * groups + k
+            arrive(unit_of(r))
+            put(r)
+        arrive(unit_of(r) + 1)
+        put_rim(h)
+    for e in range(dop_count):
+        out_ref[:, e * LANES:(e + 1) * LANES] = stage[e]
+    for copy in copies.values():
+        copy.wait_send()
+
+
+def fused_kernel(dop_count, total_batches, scale, x_hbm, *refs):
+    pieces = x_hbm.shape[3] // (FAN * PIECE)
+
+    def sums(q):
+        return tuple(pltpu.ACC(q)((PIECE, 2 * LANES), jnp.float32) for _ in range(pieces))
+
+    def run(accs):
+        fused_body(accs, dop_count, total_batches, scale, x_hbm, *refs)
+
+    pl.run_scoped(run, tuple(tuple((sums(q), sums(q)) for _ in range(2)) for q in range(2)))
+
+
+def fused(profiles, range_walk, band_order, dop_count, total_batches):
+    batches, _, delays, pulses = profiles.shape
+    bands = band_order.shape[0]
+    short = pulses // FAN
+    units = FAN + FAN // (LANES // WALK)
+    vmem = pl.BlockSpec(memory_space=pltpu.VMEM)
+    blocks = (SUB, LANES)
+    f32 = jnp.float32
+    return pl.pallas_call(
+        functools.partial(fused_kernel, dop_count, total_batches, 1.0 / (total_batches * pulses)),
+        out_shape=jax.ShapeDtypeStruct((pulses // bands, dop_count * delays), f32),
+        in_specs=[
+            pl.BlockSpec(memory_space=pl.ANY), pl.BlockSpec(memory_space=pl.ANY),
+            vmem, pl.BlockSpec(memory_space=pltpu.SMEM),
+        ],
+        out_specs=vmem,
+        scratch_shapes=[
+            pltpu.VMEM(profiles.shape, jnp.bfloat16),
+            pltpu.VMEM((FAN, short, 2 * short), jnp.bfloat16),
+            pltpu.VMEM((short, short), jnp.bfloat16),
+            pltpu.VMEM((FAN, batches // PAIR, PAIR * delays, 2 * short), jnp.bfloat16),
+            pltpu.VMEM((pulses, LANES), jnp.int32),
+            pltpu.VMEM((FAN, short // SUB, SUB, LANES), jnp.int32),
+            pltpu.VMEM((2, short // SUB, SUB, LANES), f32),
+            pltpu.VMEM((2, short // SUB, SUB, LANES), f32),
+            pltpu.VMEM((dop_count, pulses // bands, LANES), f32),
+            pltpu.VMEM((units, 2, dop_count, 2, *blocks), f32),
+            pltpu.VMEM((units, dop_count, 2, *blocks), f32),
+            pltpu.VMEM((units, dop_count, *blocks), f32),
+            pltpu.VMEM((units, dop_count, *blocks), f32),
+            pltpu.VMEM((units, dop_count, *blocks), f32),
+            pltpu.VMEM((units, dop_count, *blocks), f32),
+            pltpu.SemaphoreType.DMA((batches,)),
+            pltpu.SemaphoreType.DMA((FAN,)),
+            pltpu.SemaphoreType.DMA((units,)),
+            pltpu.SemaphoreType.DMA((units,)),
+            pltpu.SemaphoreType.DMA((units,)),
+            pltpu.SemaphoreType.DMA((units,)),
+            pltpu.SemaphoreType.DMA((units, dop_count)),
+            pltpu.SemaphoreType.DMA((units, dop_count)),
+        ],
+        compiler_params=pltpu.CompilerParams(
+            collective_id=0, has_side_effects=True, vmem_limit_bytes=60 << 20
+        ),
+    )(profiles, fan_table(pulses), range_walk.reshape(pulses // LANES, LANES), band_order)
+
+
+def fits(profiles, band_order, dop_count, slow_count, total_batches):
+    batches, _, delays, pulses = profiles.shape
+    return (
+        delays == LANES and pulses == 2 * LANES * FAN and batches % (2 * PAIR) == 0
+        and pulses == band_order.shape[0] * SUB * FAN and band_order.shape[0] == dop_count * slow_count
+        and slow_count == 4 and dop_count > 1 and power_of_two(dop_count) and power_of_two(total_batches)
+    )
+
+
 def on_device(profiles, range_walk, band_order):
     total_batches = profiles.shape[0] * lax.axis_size("slow")
     delays = profiles.shape[2]
     dop_count, slow_count = lax.axis_size("dop"), lax.axis_size("slow")
+    if fits(profiles, band_order, dop_count, slow_count, total_batches):
+        return fused(profiles, range_walk, band_order, dop_count, total_batches)
     per_band = profiles.shape[3] // (dop_count * slow_count * RADIX)
     joined = (
         delays == LANES and per_band % TILE == 0 and slow_count > 1

time: 43 us -> 34.7 us (0.81)
  Pallas kernels: 39.4 us -> 32.8 us
  local copies, waits for them, and re-layouts: 3.37 us -> 1.67 us
    pallas_call x2 -> x1, Pallas kernels: 39.4 us -> 32.8 us  [fused(): pl.pallas_call(functools.partial(fused_kernel, dop_count, total_batches,...]
    broadcast_in_dim x1 -> x0, local copies, waits for them, and re-layouts: 1.02 us -> none  [aligned_power(): walks = jnp.broadcast_to(range_walk[:, None], (pulses, LANES))]
    unnamed x5 -> x1, local copies, waits for them, and re-layouts: 2.35 us -> 1.67 us
where the time goes in v1:
time: 34.7 us; the launch traced here: 34.5 us
  Pallas kernels  32.8 us (95%)
  local copies, waits for them, and re-layouts  1.67 us (5%)
    pallas_call x1, Pallas kernels, fused(): pl.pallas_call(functools.partial(fused_kernel, dop_count, total_batches,...  32.8 us
    unnamed x1, local copies, waits for them, and re-layouts  1.67 us

profile of v1, /device:TPU:0, one launch (start us, length us, event | category | flops | bytes accessed | tf_op | source)
XLA Modules:
  0.0 34.5 jit_solution(10815238466415541003)
XLA Ops:
  0.0 32.8 %shard_map.46 = f32[64,1024]{1,0:T(8,128)} custom-call(bf16[8,2,128,2048]{3,2,1,0:T(8,128)(2,1)} %x_hbm.1, bf16[8,256,512]{2,1,0:T(8,128)(2,1)} %constant.2.clone.refs_0_, s32[16,128]{1,0:T(8,128)} %bitcast.1, s32[32]{0:T(128)} %refs_2_.1), custom_call_target="tpu_custom_call" | custom-call | tf_op jit(solution)/shard_map/pallas_call | solution.py:603
  32.8 1.7 %copy.6 = f32[64,1024]{1,0:T(8,128)} copy(f32[64,1024]{1,0:T(8,128)} %shard_map.46) | data formatting | bytes 524288

commit v2 on v1

--- a/solution.py
+++ b/solution.py
@@ -320,8 +320,11 @@
 
 
 FAN = 8
+NEAR_LAG = 1
+HOME_LAG = 5
 SUB = 8
 PIECE = 32
+ROWS = 16
 PAIR = 2
 
 
@@ -331,6 +334,16 @@
     phases = (rows * np.arange(short)) % pulses
     angles = phases.astype(np.float32) * np.float32(2.0 * math.pi / pulses)
     return jnp.asarray(np.concatenate([np.cos(angles), np.sin(angles)], axis=2), jnp.bfloat16)
+
+
+def picked(value, index):
+    dims = lax.GatherDimensionNumbers(
+        offset_dims=(), collapsed_slice_dims=(1,), start_index_map=(1,),
+        operand_batching_dims=(0,), start_indices_batching_dims=(0,),
+    )
+    return lax.gather(
+        value, index[..., None], dims, slice_sizes=(1, 1), mode=lax.GatherScatterMode.PROMISE_IN_BOUNDS
+    )
 
 
 def turned(re, im):
@@ -356,46 +369,64 @@
 
 def fused_body(
     accs, dop_count, total_batches, scale,
-    x_hbm, table_hbm, walk_ref, order_ref, out_ref,
-    x_buf, table, minus, y_buf, spun, walks, own, rim, stage,
-    held, near, passed, across, last, landed,
-    x_sem, table_sem, near_send, near_recv, across_send, across_recv, land_send, land_recv,
+    x_hbm, table_hbm, walk_hbm, order_hbm, out_ref,
+    walk_ref, order_ref, x_buf, table, y_buf, spun, walks, bases, powers, own, rim, stage,
+    edges, held, near, passed, across, last, landed,
+    small_sem, x_sem, table_sem, near_send, near_recv, across_send, across_recv, land_send, land_recv,
 ):
     batches, _, delays, pulses = x_buf.shape
     short = pulses // FAN
     pairs = batches // PAIR
-    bands = order_ref.shape[0]
+    bands = order_hbm.shape[0]
     dop, slow = lax.axis_index("dop"), lax.axis_index("slow")
     core, side = lax.rem(slow, 2), lax.div(slow, 2)
     core_peer, side_peer = (dop, flipped(slow, 1)), (dop, flipped(slow, 2))
     partners = [core_peer, side_peer] + [(flipped(dop, j), slow) for j in range(1, dop_count)]
     groups = LANES // WALK
-    units = FAN + FAN // groups
-
-    loads = [pltpu.make_async_copy(x_hbm.at[g], x_buf.at[g], x_sem.at[g]) for g in range(batches)]
-    for load in loads:
-        load.start()
-    table_loads = [
-        pltpu.make_async_copy(table_hbm.at[r], table.at[r], table_sem.at[r]) for r in range(FAN)
-    ]
-    for load in table_loads:
-        load.start()
 
     barrier = pltpu.get_barrier_semaphore()
     for partner in partners:
         pl.semaphore_signal(barrier, inc=1, device_id=partner, device_id_type=MESH)
 
+    small_loads = [
+        pltpu.make_async_copy(walk_hbm, walk_ref, small_sem.at[0]),
+        pltpu.make_async_copy(order_hbm, order_ref, small_sem.at[1]),
+    ]
+    table_load = pltpu.make_async_copy(table_hbm, table, table_sem)
+
+    def load(g):
+        return pltpu.make_async_copy(x_hbm.at[g], x_buf.at[g], x_sem.at[g])
+
+    for copy in small_loads:
+        copy.start()
+    for g in range(batches):
+        load(g).start()
+    table_load.start()
+
+    first_batch = slow * batches
+    for copy in small_loads:
+        copy.wait()
     for a in range(pulses // LANES):
         row = jnp.broadcast_to(walk_ref[a:a + 1, :], (LANES, LANES))
         spun[a * LANES:(a + 1) * LANES, :] = row.T
-    for r in range(FAN):
-        walks[r] = spun[pl.ds(r, short, stride=FAN), :].reshape(-1, SUB, LANES)
-
-    def spread(g):
+
+    @pl.loop(0, FAN)
+    def _(r):
+        walk = spun[pl.ds(r, short, stride=FAN), :]
+        base = lax.broadcasted_iota(jnp.int32, walk.shape, 1) * total_batches + walk * first_batch
+        walks[r] = walk.reshape(-1, SUB, LANES)
+        bases[r] = base.reshape(-1, SUB, LANES)
+
+    @pl.loop(0, batches)
+    def _(g):
+        load(g).wait()
+        pair = lax.div(g, PAIR)
+        first = lax.rem(g, PAIR) * delays
+
         @pl.loop(0, delays // 16)
         def _(block):
             at = pl.ds(pl.multiple_of(block * 16, 16), 16)
-            to = pl.ds(pl.multiple_of((g % PAIR) * delays + block * 16, 16), 16)
+            to = pl.ds(pl.multiple_of(first + block * 16, 16), 16)
             for lane in range(0, short, LANES):
                 parts = [
                     [
@@ -405,95 +436,142 @@
                     for c in range(2)
                 ]
                 for r, (re, im) in enumerate(turned(*parts)):
-                    y_buf[r, g // PAIR, to, lane:lane + LANES] = re.astype(jnp.bfloat16)
-                    y_buf[r, g // PAIR, to, short + lane:short + lane + LANES] = im.astype(jnp.bfloat16)
-
-    for g in range(batches):
-        loads[g].wait()
-        spread(g)
-
-    lane = lax.broadcasted_iota(jnp.int32, (PIECE, LANES), 1)
+                    y_buf[r, pair, to, lane:lane + LANES] = re.astype(jnp.bfloat16)
+                    y_buf[r, pair, to, short + lane:short + lane + LANES] = im.astype(jnp.bfloat16)
+
     thin = lax.broadcasted_iota(jnp.int32, (SUB, LANES), 1)
     shift = total_batches.bit_length() - 1
-    lanes = lane * total_batches
-    first_batch = slow * batches
     pieces = short // PIECE
-
-    def align(r, half, piece, specs):
-        at = slice(piece * PIECE // SUB, (piece + 1) * PIECE // SUB)
-        walk = walks[r, at].reshape(PIECE, LANES)
-        own_add, rim_add = None, None
-        for q, (re, im) in enumerate(specs):
-            power = re * re + im * im
-            for b in range(PAIR):
-                batch = first_batch + (2 * half + q) * PAIR + b
-                source = lax.shift_right_arithmetic(lanes + walk * batch, shift)
-                wrapped = source & (LANES - 1)
-                value = jnp.take_along_axis(
-                    power[:, b * LANES:(b + 1) * LANES], wrapped, axis=1, mode="promise_in_bounds"
-                )
-                inside = source == wrapped
-                kept, spilled = jnp.where(inside, value, 0.0), jnp.where(inside, 0.0, value)
-                own_add = kept if own_add is None else own_add + kept
-                rim_add = spilled if rim_add is None else rim_add + spilled
-        if half:
-            own_add += own[r % 2, at].reshape(PIECE, LANES)
-            rim_add += rim[r % 2, at].reshape(PIECE, LANES)
-        own[r % 2, at] = own_add.reshape(-1, SUB, LANES)
-        rim[r % 2, at] = rim_add.reshape(-1, SUB, LANES)
+    halves = pairs // 2
+
+    def multiply(r, half):
+        for q in range(2):
+            pltpu.matmul_push_rhs(y_buf[r, 2 * half + q, :, :short], 0, q, transpose=True)
+        for q in range(2):
+            pltpu.matmul_push_rhs(y_buf[r, 2 * half + q, :, short:], 1, q, transpose=True)
+        for register, columns in ((0, (0, 1, 1)), (1, (1, 0, -1))):
+            for piece in range(pieces):
+                rows = slice(piece * PIECE, (piece + 1) * PIECE)
+                first = table[r, rows, columns[0] * short:(columns[0] + 1) * short]
+                second = table[r, rows, columns[1] * short:(columns[1] + 1) * short]
+                if columns[2] < 0:
+                    second = -second
+                for q in range(2):
+                    re_accs, im_accs = accs[q][half % 2]
+                    pltpu.matmul_acc_lhs(
+                        re_accs[piece], first, load_staged_rhs=register if piece == 0 else None
+                    )
+                    pltpu.matmul_acc_lhs(im_accs[piece], second)
+
+    def measure(half):
+        for piece in range(pieces):
+            for q in range(2):
+                re, im = (pltpu.matmul_pop(sums[piece]) for sums in accs[q][half % 2])
+                powers[half % 2, q, piece * PIECE:(piece + 1) * PIECE, :] = re * re + im * im
+
+    def align(r, half):
+        for piece in range(short // ROWS):
+            at = slice(piece * ROWS // SUB, (piece + 1) * ROWS // SUB)
+            walk = walks[r, at].reshape(ROWS, LANES)
+            moved = bases[r, at].reshape(ROWS, LANES)
+            if half:
+                moved += walk * (2 * PAIR * half)
+            own_add, rim_add = None, None
+            for q in range(2):
+                for b in range(PAIR):
+                    if q or b:
+                        moved += walk
+                    power = powers[half % 2, q, piece * ROWS:(piece + 1) * ROWS, b * LANES:(b + 1) * LANES]
+                    source = lax.shift_right_arithmetic(moved, shift)
+                    wrapped = source & (LANES - 1)
+                    value = picked(power, wrapped)
+                    inside = source == wrapped
+                    kept, spilled = jnp.where(inside, value, 0.0), jnp.where(inside, 0.0, value)
+                    own_add = kept if own_add is None else own_add + kept
+                    rim_add = spilled if rim_add is None else rim_add + spilled
+            if half:
+                own_add += own[at].reshape(ROWS, LANES)
+                rim_add += rim[at].reshape(ROWS, LANES)
+            own[at] = own_add.reshape(-1, SUB, LANES)
+            rim[at] = rim_add.reshape(-1, SUB, LANES)
 
     def slot(band):
         owner_dop, owner_slow = divmod(band, 4)
         return owner_slow % 2, owner_dop, owner_slow // 2
 
-    copies = {}
-
-    def send(key, source, target, sent, received, device):
-        copies[key] = pltpu.make_async_remote_copy(
+    def pack(r):
+        h, k = lax.div(r, groups), lax.rem(r, groups)
+        mask = lax.shift_right_logical(thin, WALK.bit_length() - 1) == k
+        for band in range(bands):
+            source = order_ref[band]
+            c, d, s = slot(band)
+            held[r, c, d, s] = own[source]
+            edge = rim[source]
+            folded = edge + pltpu.roll(edge, WALK, 1)
+            value = pltpu.roll(folded, k * WALK, 1)
+            edges[c, d, s] = jnp.where(mask, value, edges[c, d, s])
+
+        @pl.when(k == groups - 1)
+        def _():
+            held[FAN + h] = edges[...]
+
+    def remote(source, target, sent, received, device):
+        return pltpu.make_async_remote_copy(
             src_ref=source, dst_ref=target, send_sem=sent, recv_sem=received,
             device_id=device, device_id_type=MESH,
         )
-        copies[key].start()
-
-    def send_near(u):
-        send(("near", u), held.at[u, 1 - core], near.at[u], near_send.at[u], near_recv.at[u], core_peer)
+
+    def near_copy(u):
+        return remote(held.at[u, 1 - core], near.at[u], near_send, near_recv.at[u], core_peer)
+
+    def across_copy(u):
+        return remote(passed.at[u], across.at[u], across_send, across_recv.at[u], side_peer)
+
+    def home_copy(u, j):
+        return remote(
+            last.at[u, j], landed.at[u, j], land_send, land_recv.at[u], (flipped(dop, j), slow)
+        )
+
+    def arrive(u):
+        others = pl.ds(1, dop_count - 1)
+        remote(last.at[u, others], landed.at[u, others], land_send, land_recv.at[u], core_peer).wait_recv()
 
     def send_across(u):
-        copies["near", u].wait_recv()
+        near_copy(u).wait_recv()
         for d in range(dop_count):
             passed[u, d] = held[u, core, d, 1 - side] + near[u, d, 1 - side]
-        send(
-            ("across", u), passed.at[u], across.at[u], across_send.at[u], across_recv.at[u], side_peer
-        )
+        across_copy(u).start()
 
     def send_home(u):
-        copies["across", u].wait_recv()
+        across_copy(u).wait_recv()
         for j in range(dop_count - 1, -1, -1):
             d = flipped(dop, j)
             total = held[u, core, d, side] + near[u, d, side] + across[u, d]
             if j:
                 last[u, j] = total
-                send(
-                    ("home", u, j), last.at[u, j], landed.at[u, j],
-                    land_send.at[u, j], land_recv.at[u, j], (d, slow),
-                )
+                home_copy(u, j).start()
             else:
                 landed[u, 0] = total
 
-    def arrive(u):
-        for j in range(dop_count - 1, 0, -1):
-            copies["home", u, j].wait_recv()
-
-    def unit_of(r):
-        return r + r // groups
+    def both(step, r):
+        step(r)
+        if isinstance(r, int):
+            if r % groups == groups - 1:
+                step(FAN + r // groups)
+        else:
+            @pl.when(lax.rem(r, groups) == groups - 1)
+            def _():
+                step(FAN + lax.div(r, groups))
 
     def put(r):
+        arrive(r)
         for e in range(dop_count):
-            stage[e, pl.ds(r, SUB, stride=FAN), :] = landed[unit_of(r), flipped(dop, e)]
+            stage[e, pl.ds(r, SUB, stride=FAN), :] = landed[r, flipped(dop, e)]
 
     def put_rim(h):
+        u = FAN + h
+        arrive(u)
         mine = order_ref[dop * 4 + slow]
-        u = h * (groups + 1) + groups
         for k in range(groups):
             r = h * groups + k
             walk = walks[r, mine]
@@ -510,74 +588,53 @@
                 at = (e, pl.ds(r, SUB, stride=FAN), slice(None))
                 stage[at] = stage[at] + add
 
-    def pack(r):
-        u = unit_of(r)
-        k = r % groups
-        for band in range(bands):
-            source = order_ref[band]
-            c, d, s = slot(band)
-            held[u, c, d, s] = own[r % 2, source] * scale
-            edge = rim[r % 2, source] * scale
-            left = pltpu.roll(edge, k * WALK, 1) if k else edge
-            right = pltpu.roll(edge, (k * WALK + WALK) % LANES, 1) if (k + 1) % groups else edge
-            mask = jnp.logical_and(thin >= k * WALK, thin < (k + 1) * WALK)
-            value = jnp.where(mask, left + right, 0.0)
-            v = (r // groups) * (groups + 1) + groups
-            held[v, c, d, s] = value if k == 0 else held[v, c, d, s] + value
-
-    for r in range(FAN):
-        table_loads[r].wait()
-        minus[...] = -table[r, :, :short]
-        for half in range(pairs // 2):
-            for q in range(2):
-                p = 2 * half + q
-                re_accs, im_accs = accs[q][half % 2]
-                pltpu.matmul_push_rhs(y_buf[r, p, :, :short], 0, q, transpose=True)
-                pltpu.matmul_push_rhs(y_buf[r, p, :, short:], 1, q, transpose=True)
-                for piece in range(pieces):
-                    rows = slice(piece * PIECE, (piece + 1) * PIECE)
-                    pltpu.matmul_acc_lhs(
-                        re_accs[piece], table[r, rows, :short], load_staged_rhs=0 if piece == 0 else None
-                    )
-                    pltpu.matmul_acc_lhs(im_accs[piece], table[r, rows, short:])
-                for piece in range(pieces):
-                    rows = slice(piece * PIECE, (piece + 1) * PIECE)
-                    pltpu.matmul_acc_lhs(
-                        re_accs[piece], table[r, rows, short:], load_staged_rhs=1 if piece == 0 else None
-                    )
-                    pltpu.matmul_acc_lhs(im_accs[piece], minus[rows, :])
-            for piece in range(pieces):
-                specs = []
-                for q in range(2):
-                    re_accs, im_accs = accs[q][half % 2]
-                    specs.append((pltpu.matmul_pop(re_accs[piece]), pltpu.matmul_pop(im_accs[piece])))
-                align(r, half, piece, specs)
+    def finish(r):
+        put(r)
+        if r % groups == groups - 1:
+            put_rim(r // groups)
+
+    edges[...] = jnp.zeros(edges.shape, edges.dtype)
+    table_load.wait()
+    multiply(0, 0)
+    measure(0)
+    pl.semaphore_wait(barrier, len(partners))
+
+    @pl.loop(0, FAN)
+    def _(r):
+        for half in range(halves):
+            if half + 1 < halves:
+                multiply(r, half + 1)
+            else:
+                multiply(lax.rem(r + 1, FAN), 0)
+            measure((half + 1) % halves)
+            align(r, half)
         pack(r)
-        if r == 0:
-            pl.semaphore_wait(barrier, len(partners))
-        send_near(unit_of(r))
-        if r % groups == groups - 1:
-            send_near(unit_of(r) + 1)
-        if r >= 1:
-            send_across(unit_of(r - 1))
-            if (r - 1) % groups == groups - 1:
-                send_across(unit_of(r - 1) + 1)
-
-    for u in range(unit_of(FAN - 1), units):
-        send_across(u)
-    for u in range(units):
-        send_home(u)
-    for h in range(FAN // groups):
-        for k in range(groups):
-            r = h * groups + k
-            arrive(unit_of(r))
-            put(r)
-        arrive(unit_of(r) + 1)
-        put_rim(h)
+        both(lambda u: near_copy(u).start(), r)
+
+        @pl.when(r >= NEAR_LAG)
+        def _():
+            both(send_across, r - NEAR_LAG)
+
+        @pl.when(r >= HOME_LAG)
+        def _():
+            both(send_home, r - HOME_LAG)
+
+    for r in range(FAN - NEAR_LAG, FAN):
+        both(send_across, r)
+    for r in range(FAN - HOME_LAG, FAN):
+        both(send_home, r)
+        if r < FAN - 1:
+            finish(r - FAN + HOME_LAG)
+    for r in range(HOME_LAG - 1, FAN):
+        finish(r)
     for e in range(dop_count):
-        out_ref[:, e * LANES:(e + 1) * LANES] = stage[e]
-    for copy in copies.values():
-        copy.wait_send()
+        out_ref[:, e * LANES:(e + 1) * LANES] = stage[e] * scale
+    others = pl.ds(1, dop_count - 1)
+    remote(held.at[:, 0], near, near_send, near_recv.at[0], core_peer).wait_send()
+    remote(passed, across, across_send, across_recv.at[0], side_peer).wait_send()
+    remote(
+        last.at[:, others], landed.at[:, others], land_send, land_recv.at[0], core_peer
+    ).wait_send()
 
 
 def fused_kernel(dop_count, total_batches, scale, x_hbm, *refs):
@@ -603,40 +660,45 @@
     return pl.pallas_call(
         functools.partial(fused_kernel, dop_count, total_batches, 1.0 / (total_batches * pulses)),
         out_shape=jax.ShapeDtypeStruct((pulses // bands, dop_count * delays), f32),
-        in_specs=[
-            pl.BlockSpec(memory_space=pl.ANY), pl.BlockSpec(memory_space=pl.ANY),
-            vmem, pl.BlockSpec(memory_space=pltpu.SMEM),
-        ],
+        in_specs=[pl.BlockSpec(memory_space=pltpu.HBM)] * 4,
         out_specs=vmem,
         scratch_shapes=[
+            pltpu.VMEM((pulses // LANES, LANES), jnp.int32),
+            pltpu.SMEM((bands,), jnp.int32),
             pltpu.VMEM(profiles.shape, jnp.bfloat16),
             pltpu.VMEM((FAN, short, 2 * short), jnp.bfloat16),
-            pltpu.VMEM((short, short), jnp.bfloat16),
             pltpu.VMEM((FAN, batches // PAIR, PAIR * delays, 2 * short), jnp.bfloat16),
             pltpu.VMEM((pulses, LANES), jnp.int32),
             pltpu.VMEM((FAN, short // SUB, SUB, LANES), jnp.int32),
-            pltpu.VMEM((2, short // SUB, SUB, LANES), f32),
-            pltpu.VMEM((2, short // SUB, SUB, LANES), f32),
+            pltpu.VMEM((FAN, short // SUB, SUB, LANES), jnp.int32),
+            pltpu.VMEM((2, 2, short, PAIR * LANES), f32),
+            pltpu.VMEM((short // SUB, SUB, LANES), f32),
+            pltpu.VMEM((short // SUB, SUB, LANES), f32),
             pltpu.VMEM((dop_count, pulses // bands, LANES), f32),
+            pltpu.VMEM((2, dop_count, 2, *blocks), f32),
             pltpu.VMEM((units, 2, dop_count, 2, *blocks), f32),
             pltpu.VMEM((units, dop_count, 2, *blocks), f32),
             pltpu.VMEM((units, dop_count, *blocks), f32),
             pltpu.VMEM((units, dop_count, *blocks), f32),
             pltpu.VMEM((units, dop_count, *blocks), f32),
             pltpu.VMEM((units, dop_count, *blocks), f32),
+            pltpu.SemaphoreType.DMA((2,)),
             pltpu.SemaphoreType.DMA((batches,)),
-            pltpu.SemaphoreType.DMA((FAN,)),
+            pltpu.SemaphoreType.DMA,
+            pltpu.SemaphoreType.DMA,
             pltpu.SemaphoreType.DMA((units,)),
+            pltpu.SemaphoreType.DMA,
             pltpu.SemaphoreType.DMA((units,)),
+            pltpu.SemaphoreType.DMA,
             pltpu.SemaphoreType.DMA((units,)),
-            pltpu.SemaphoreType.DMA((units,)),
-            pltpu.SemaphoreType.DMA((units, dop_count)),
-            pltpu.SemaphoreType.DMA((units, dop_count)),
         ],
         compiler_params=pltpu.CompilerParams(
-            collective_id=0, has_side_effects=True, vmem_limit_bytes=60 << 20
+            collective_id=0, has_side_effects=True, vmem_limit_bytes=48 << 20
         ),
-    )(profiles, fan_table(pulses), range_walk.reshape(pulses // LANES, LANES), band_order)
+    )(*(
+        pltpu.with_memory_space_constraint(value, pltpu.HBM)
+        for value in (profiles, fan_table(pulses), range_walk.reshape(pulses // LANES, LANES), band_order)
+    ))
 
 
 def fits(profiles, band_order, dop_count, slow_count, total_batches):

time: 34.7 us -> 30.2 us (0.87)
  Pallas kernels: 32.8 us -> 29.4 us
  local copies, waits for them, and re-layouts: 1.67 us -> 0.71 us
    pallas_call x1, Pallas kernels: 32.8 us -> 29.4 us  [fused(): pl.pallas_call(functools.partial(fused_kernel, dop_count, total_batches,...]
    unnamed x1, local copies, waits for them, and re-layouts: 1.67 us -> 0.71 us
where the time goes in v2:
time: 30.2 us; the launch traced here: 30.1 us
  Pallas kernels  29.4 us (97%)
  local copies, waits for them, and re-layouts  0.71 us (2%)
    pallas_call x1, Pallas kernels, fused(): pl.pallas_call(functools.partial(fused_kernel, dop_count, total_batches,...  29.4 us
    unnamed x1, local copies, waits for them, and re-layouts  0.71 us

profile of v2, /device:TPU:0, one launch (start us, length us, event | category | flops | bytes accessed | tf_op | source)
XLA Modules:
  0.0 30.1 jit_solution(12994670475346180835)
XLA Ops:
  0.0 29.4 %shard_map.46 = f32[64,1024]{1,0:T(8,128)S(1)} custom-call(bf16[8,2,128,2048]{3,2,1,0:T(8,128)(2,1)} %x_hbm.1, bf16[8,256,512]{2,1,0:T(8,128)(2,1)} %constant.2.clone.refs_0_, s32[16,128]{1,0:T(8,128)} %bitcast.1, s32[32]{0:T(128)} %refs_2_.1), custom_call_target="tpu_custom_call" | custom-call | tf_op jit(solution)/shard_map/pallas_call | solution.py:660
  29.4 0.7 %copy.6 = f32[64,1024]{1,0:T(8,128)} copy(f32[64,1024]{1,0:T(8,128)S(1)} %shard_map.46) | data formatting | bytes 524288
